TPU v7x, 32 devices: a whole 2x2x4 slice. The times are simulated.
32 devices in a mesh: seq: 8 (over y, x, core), tp: 4 (over z).
Axes of the slice: x: 2, y: 2, z: 4, core: 2. Of those that a mesh axis runs over, the one named last changes fastest.
Arguments:
- hidden_in: bfloat16 [4096, 2048], P('seq', 'tp'), may hold values from -60 to 60
- w_query: bfloat16 [2048, 2048], P(None, 'tp'), may hold values from -0.125 to 0.125
- w_key: bfloat16 [2048, 2048], P(None, 'tp'), may hold values from -0.125 to 0.125
- w_value: bfloat16 [2048, 2048], P(None, 'tp'), may hold values from -0.8984375 to 0.8984375
- w_pos: bfloat16 [2048, 2048], P(None, 'tp'), may hold values from -0.125 to 0.125
- w_out: bfloat16 [2048, 2048], P('tp'), may hold values from -0.125 to 0.125
- bias_content: float32 [16, 128], P('tp'), may hold values from -4 to 4
- bias_pos: float32 [16, 128], P('tp'), may hold values from -4 to 4
- norm_gain: float32 [2048], P('tp'), may hold values from 0.1 to 1.9
- norm_bias: float32 [2048], P('tp'), may hold values from -3 to 3
Outputs:
- hidden_out: bfloat16 [4096, 2048], P('seq', 'tp')
All inputs are finite; a program needn't handle non-finite values.
Results may differ from a plain program's by a relative error of at most 0.014.
The roundings to bfloat16 on the way count: a program that leaves them out, or rounds other values in their place, can miss the bound.
Values may be sent and summed in bfloat16 or wider, within the bound.
No kernel may reach another device: no remote copies, remote signals or barrier semaphores. Data moves between devices by JAX's collectives and lax.ppermute only.
A program may use at most 128 MiB of HBM per device.

v0:
```python
import jax
import jax.numpy as jnp
from jax import lax
from jax.sharding import PartitionSpec as P


def shifted(block, axis, distance):
    devices = range(lax.axis_size(axis))
    route = [(i - distance, i) for i in devices if i - distance in devices]
    return lax.ppermute(block, axis, route)


def relative_table(span, width):
    half = width // 2
    freq = jnp.exp(-jnp.log(10000.0) * jnp.arange(half).astype(jnp.float32) / half)
    distance = (span - 1 - jnp.arange(span)).astype(jnp.float32)
    angle = distance[:, None] * freq[None, :]
    return jnp.concatenate([jnp.sin(angle), jnp.cos(angle)], 1).astype(jnp.bfloat16)


def shift_rows(table, seg, span):
    heads = table.shape[0]
    padded = jnp.pad(table, ((0, 0), (0, 0), (0, 1)))
    flat = padded.reshape(heads, seg * (span + 1))
    return flat[:, seg - 1 : seg - 1 + seg * span].reshape(heads, seg, span)


def shards(
    hidden_in, w_query, w_key, w_value, w_pos, w_out, bias_content, bias_pos, norm_gain, norm_bias
):
    seg = hidden_in.shape[0]
    heads = bias_content.shape[0]
    head_dim = bias_content.shape[1]
    width = heads * head_dim
    model_width = w_query.shape[0]
    span = 3 * seg
    memory = 2 * seg
    place = lax.axis_index("seq")
    own = lax.all_gather(hidden_in, "tp", axis=1, tiled=True)
    query = jnp.dot(own, w_query, preferred_element_type=jnp.float32).astype(jnp.bfloat16)
    own_keys = jnp.dot(own, w_key, preferred_element_type=jnp.float32).astype(jnp.bfloat16)
    own_values = jnp.dot(own, w_value, preferred_element_type=jnp.float32).astype(jnp.bfloat16)
    key_parts = []
    value_parts = []
    for distance in (2, 1):
        earlier_keys, earlier_values = shifted((own_keys, own_values), "seq", distance)
        key_parts.append(earlier_keys)
        value_parts.append(earlier_values)
    keys = jnp.concatenate(key_parts + [own_keys], 0)
    values = jnp.concatenate(value_parts + [own_values], 0)
    rel = jnp.dot(
        relative_table(span, model_width), w_pos, preferred_element_type=jnp.float32
    ).astype(jnp.bfloat16)
    rel = rel.reshape(span, heads, head_dim)
    keys = keys.reshape(span, heads, head_dim)
    values = values.reshape(span, heads, head_dim)
    q_rows = query.astype(jnp.float32).reshape(seg, heads, head_dim)
    content_q = (q_rows + bias_content[None]).astype(jnp.bfloat16)
    pos_q = (q_rows + bias_pos[None]).astype(jnp.bfloat16)
    content = jnp.einsum("ihd,jhd->hij", content_q, keys, preferred_element_type=jnp.float32)
    position = jnp.einsum("ihd,ehd->hie", pos_q, rel, preferred_element_type=jnp.float32)
    position = shift_rows(position, seg, span)
    score = (content + position) * (1.0 / jnp.sqrt(jnp.float32(head_dim)))
    row = jnp.arange(seg)[:, None]
    col = jnp.arange(span)[None, :]
    allowed = (col <= row + memory) & (place * seg - memory + col >= 0)
    score = jnp.where(allowed[None], score, jnp.float32(-1e30))
    probs = jax.nn.softmax(score, axis=-1).astype(jnp.bfloat16)
    attended = jnp.einsum("hij,jhd->ihd", probs, values, preferred_element_type=jnp.float32)
    attended = attended.astype(jnp.bfloat16).reshape(seg, width)
    partial_out = jnp.dot(attended, w_out, preferred_element_type=jnp.float32)
    branch = lax.psum_scatter(
        partial_out.astype(jnp.bfloat16), "tp", scatter_dimension=1, tiled=True
    ).astype(jnp.float32)
    summed = hidden_in.astype(jnp.float32) + branch
    total = lax.psum(jnp.sum(summed, axis=1), "tp")
    center = total / model_width
    centred = summed - center[:, None]
    spread = lax.psum(jnp.sum(centred * centred, axis=1), "tp") / model_width
    normed = centred / jnp.sqrt(spread[:, None] + 1e-05)
    return (normed * norm_gain[None] + norm_bias[None]).astype(jnp.bfloat16)


def solution(mesh):
    in_specs = (
        P("seq", "tp"),
        P(None, "tp"),
        P(None, "tp"),
        P(None, "tp"),
        P(None, "tp"),
        P("tp", None),
        P("tp", None),
        P("tp", None),
        P("tp"),
        P("tp"),
    )
    out_specs = P("seq", "tp")
    return jax.shard_map(shards, mesh=mesh, in_specs=in_specs, out_specs=out_specs, check_vma=False)
```

profile of v0, /device:TPU:0, one launch (start us, length us, event | category | flops | bytes accessed | tf_op | source)
XLA Modules:
  0.0 256.7 jit_solution(2363888968351827985)
XLA Ops:
  6.5 0.7 all-gather.2.cloned.1.call-update
  7.3 0.0 reduce-scatter.2.cloned.1.call-start
  7.4 0.6 fusion.10
  8.0 23.2 %fusion.3 = (bf16[1536,1024]{1,0:T(8,128)(2,1)S(1)}, bf16[1536,1024]{1,0:T(8,128)(2,1)S(1)}) fusion(f32[1024]{0:T(1024)S(1)} %multiply_exponential_fusion, f32[1536]{0:T(1024)S(1)} %subtract_convert_fusion), kind=kLoop, calls=%fused_computation.8 | loop fusion | flops 4718592 | bytes 6301696 | tf_op jit(solution)/shard_map/convert.1
  31.2 4.8 %fusion.11 = bf16[1536,512]{0,1:T(8,128)(2,1)} fusion(bf16[2048,512]{1,0:T(8,128)(2,1)S(1)} %copy-done.7, bf16[1536,1024]{1,0:T(8,128)(2,1)S(1)} %get-tuple-element.6, bf16[1536,1024]{1,0:T(8,128)(2,1)S(1)} %get-tuple-element.5), kind=kOutput, calls=%fused_computation.17 | convolution fusion | flops 3234594816 | bytes 9961472 | tf_op jit(solution)/shard_map/dot_general | solution.py:51
  36.1 21.3 %all-gather.2.cloned.1.call-done = bf16[512,2048]{1,0:T(8,128)(2,1)} async-done(((bf16[512,512]{1,0:T(8,128)(2,1)}), bf16[512,2048]{1,0:T(8,128)(2,1)}) %all-gather.2.cloned.1.call-update) | async-done | bytes 2097168 | tf_op jit(solution)/shard_map/all_gather | solution.py:39
  57.3 3.6 %convolution_convert_fusion.1 = bf16[512,512]{1,0:T(8,128)(2,1)S(1)} fusion(bf16[512,2048]{1,0:T(8,128)(2,1)} %all-gather.2.cloned.1.call-done, bf16[2048,512]{1,0:T(8,128)(2,1)} %param.12), kind=kOutput, calls=%fused_computation.23 | convolution fusion | flops 1074003968 | bytes 4718592 | tf_op jit(solution)/shard_map/dot_general | solution.py:41
  61.0 4.3 %collective-permute-start.2 = (bf16[512,512]{1,0:T(8,128)(2,1)S(1)}, bf16[512,512]{1,0:T(8,128)(2,1)}, u32[]{:S(2)}, u32[]{:S(2)}) collective-permute-start(bf16[512,512]{1,0:T(8,128)(2,1)S(1)} %convolution_convert_fusion.1), channel_id=1, source_target_pairs={{0,8},{4,12},{8,16},{12,20},{16,24},{20,28},{1,9},{5,13},{9,17},{1... | collective-permute-start | bytes 1572872 | tf_op jit(solution)/shard_map/ppermute | solution.py:10
  65.3 2.1 collective-permute-start.3
  67.4 2.0 convolution_convert_fusion.3
  69.4 3.3 %collective-permute-start = (bf16[512,512]{1,0:T(8,128)(2,1)}, bf16[512,512]{1,0:T(8,128)(2,1)}, u32[]{:S(2)}, u32[]{:S(2)}) collective-permute-start(bf16[512,512]{1,0:T(8,128)(2,1)} %convolution_convert_fusion.3), channel_id=1, source_target_pairs={{0,8},{4,12},{8,16},{12,20},{16,24},{20,28},{1,9},{5,13},{9,17},{1... | collective-permute-start | bytes 1572872 | tf_op jit(solution)/shard_map/ppermute | solution.py:10
  72.8 4.0 %collective-permute-start.1 = (bf16[512,512]{1,0:T(8,128)(2,1)}, bf16[512,512]{1,0:T(8,128)(2,1)}, u32[]{:S(2)}, u32[]{:S(2)}) collective-permute-start(bf16[512,512]{1,0:T(8,128)(2,1)} %convolution_convert_fusion.3), channel_id=1, source_target_pairs={{0,4},{4,8},{8,12},{12,16},{16,20},{20,24},{24,28},{1,5},{5,9},{9,... | collective-permute-start | bytes 1572872 | tf_op jit(solution)/shard_map/ppermute | solution.py:10
  76.8 2.1 convolution_convert_fusion.2
  78.9 2.2 copy.16
  81.1 8.1 %fusion.19 = f32[4,512,1536]{2,1,0:T(8,128)} fusion(bf16[1536,4,128]{0,2,1:T(8,128)(2,1)} %bitcast.35, f32[512,4,128]{2,0,1:T(8,128)} %copy.16, f32[4,128]{1,0:T(4,128)S(1)} %copy-done.3), kind=kOutput, calls=%fused_computation.34 | convolution fusion | flops 805830656 | bytes 15206400 | tf_op jit(solution)/shard_map/ihd,ehd->hie/dot_general | solution.py:61
  89.2 10.7 %pad.4 = f32[4,512,1537]{2,1,0:T(8,128)} pad(f32[4,512,1536]{2,1,0:T(8,128)} %fusion.19, f32[]{:T(128)} %constant.13.clone.1), padding=0_0x0_0x0_1 | pad | bytes 25174020 | tf_op jit(solution)/shard_map/jit(_pad)/pad | solution.py:23
  99.9 20.2 %reshape.101 = f32[3147776]{0:T(1024)} reshape(f32[4,512,1537]{2,1,0:T(8,128)} %pad.4) | data formatting | bytes 25182208
  120.1 15.0 %reshape.96 = f32[4,786944]{1,0:T(4,128)} reshape(f32[3147776]{0:T(1024)} %reshape.101) | data formatting | bytes 25182208 | tf_op jit(solution)/shard_map/reshape | solution.py:24
  135.1 9.7 %slice.4 = f32[4,786432]{1,0:T(4,128)S(1)} slice(f32[4,786944]{1,0:T(4,128)} %reshape.96), slice={[0:4], [511:786943]} | slice | bytes 25165824 | tf_op jit(solution)/shard_map/slice | solution.py:25
  144.8 11.5 %fusion.2 = f32[4,512,1536]{2,1,0:T(8,128)} fusion(f32[1,4,512,1536]{3,1,2,0:T(4,128)S(1)} %bitcast.34, pred[512,1536]{1,0:T(8,128)(4,1)S(1)} %fusion.10, f32[512,4,128]{2,0,1:T(8,128)S(1)} %copy-done.1, f32[4,128]{1,0:T(4,128)S(1)} %copy-done.4, bf16[512,512]{1,0:T(8,128)(2,1)S(1)} %convolution_convert_fusion.1, ...), kind=kOutput, calls=%fused_computation.3 | convolution fusion | flops 819986432 | bytes 28575744 | tf_op jit(solution)/shard_map/ihd,jhd->hij/dot_general | solution.py:60
  156.3 10.4 %fusion.24 = f32[4,512]{1,0:T(4,128)S(1)} fusion(f32[4,512,1536]{2,1,0:T(8,128)} %fusion.2), kind=kOutput, calls=%fused_computation.45 | output fusion | flops 6292991 | bytes 12591104 | tf_op jit(solution)/shard_map/sub | solution.py:68
  166.8 2.6 %pad_maximum_fusion = bf16[1536,512]{1,0:T(8,128)(2,1)} fusion(bf16[512,512]{1,0:T(8,128)(2,1)} %convolution_convert_fusion.3, bf16[512,512]{1,0:T(8,128)(2,1)} %collective-permute-done.1, bf16[512,512]{1,0:T(8,128)(2,1)} %collective-permute-done), kind=kLoop, calls=%fused_computation.21 | loop fusion | flops 4718592 | bytes 3145728 | tf_op jit(solution)/shard_map/concatenate | solution.py:50
  169.4 2.6 %copy.22 = bf16[1536,512]{0,1:T(8,128)(2,1)} copy(bf16[1536,512]{1,0:T(8,128)(2,1)} %pad_maximum_fusion) | data formatting | bytes 3145728 | tf_op jit(solution)/shard_map/reshape | solution.py:56
  172.0 10.9 %fusion.16 = bf16[4,128,512]{2,1,0:T(8,128)(2,1)S(1)} fusion(bf16[1536,4,128]{0,2,1:T(8,128)(2,1)} %bitcast.36, f32[4,512]{1,0:T(4,128)S(1)} %fusion.24, f32[4,512,1536]{2,1,0:T(8,128)} %fusion.2), kind=kOutput, calls=%fused_computation.26 | convolution fusion | flops 815009280 | bytes 14688256 | tf_op jit(solution)/shard_map/hij,jhd->ihd/dot_general | solution.py:69
  182.9 2.6 %convolution_convert_fusion = bf16[512,2048]{1,0:T(8,128)(2,1)} fusion(bf16[512,512]{0,1:T(8,128)(2,1)S(1)} %bitcast.38, bf16[512,2048]{1,0:T(8,128)(2,1)S(1)} %copy-done), kind=kOutput, calls=%fused_computation.18 | convolution fusion | flops 1074790400 | bytes 4718592 | tf_op jit(solution)/shard_map/dot_general | solution.py:71
  185.6 0.0 reduce-scatter.2.cloned.1.call-update
  185.6 40.8 %reduce-scatter.2.cloned.1.call-done = bf16[512,512]{1,0:T(8,128)(2,1)} async-done(((bf16[512,2048]{1,0:T(8,128)(2,1)}), bf16[512,512]{1,0:T(8,128)(2,1)}) %reduce-scatter.2.cloned.1.call-update) | async-done | bytes 524304 | tf_op jit(solution)/shard_map/reduce_scatter | solution.py:72
  226.4 1.3 fusion.18
  227.6 10.2 %psum.14 = f32[512]{0:T(512)S(1)} all-reduce(f32[512]{0:T(512)S(1)} %fusion.18), channel_id=1, replica_groups=mesh['seq'=8,'tp'=4] {'tp'}, use_global_device_ids=true, to_apply=%region_4.5 | all-reduce | flops 512 | bytes 4096 | tf_op jit(solution)/shard_map/psum | solution.py:76
  237.8 1.3 multiply_reduce_fusion
  239.1 8.6 %psum.15 = f32[512]{0:T(512)S(1)} all-reduce(f32[512]{0:T(512)S(1)} %multiply_reduce_fusion), channel_id=1, replica_groups=mesh['seq'=8,'tp'=4] {'tp'}, use_global_device_ids=true, to_apply=%region_6.7 | all-reduce | flops 512 | bytes 4096 | tf_op jit(solution)/shard_map/psum | solution.py:79
  247.7 2.1 add_convert_fusion
  (33 shorter events, 0.1 us)
Async XLA Ops:
  6.5 176.4 %copy-start = (bf16[512,2048]{1,0:T(8,128)(2,1)S(1)}, bf16[512,2048]{1,0:T(8,128)(2,1)}, u32[]{:S(2)}) copy-start(bf16[512,2048]{1,0:T(8,128)(2,1)} %param.15) | copy-start | bytes 6291460
  6.5 50.8 %all-gather.2.cloned.1.call-start = ((), (), s32[]{:S(2)}) async-start(), calls=%async_computation.1 | async-start | bytes 2621440 | tf_op jit(solution)/shard_map/all_gather | solution.py:39
  7.3 219.1 %reduce-scatter.2.cloned.1.call-start = ((), (), s32[]{:S(2)}) async-start(), calls=%async_computation.2 | async-start | bytes 2621440 | tf_op jit(solution)/shard_map/reduce_scatter | solution.py:72
  7.9 23.3 %copy-start.7 = (bf16[2048,512]{1,0:T(8,128)(2,1)S(1)}, bf16[2048,512]{1,0:T(8,128)(2,1)}, u32[]{:S(2)}) copy-start(bf16[2048,512]{1,0:T(8,128)(2,1)} %param.14) | copy-start | bytes 6291460
  57.3 10.1 %copy-start.8 = (bf16[2048,512]{1,0:T(8,128)(2,1)S(1)}, bf16[2048,512]{1,0:T(8,128)(2,1)}, u32[]{:S(2)}) copy-start(bf16[2048,512]{1,0:T(8,128)(2,1)} %param.13) | copy-start | bytes 6291460
  57.3 10.1 %copy-start.10 = (bf16[512,2048]{1,0:T(8,128)(2,1)S(1)}, bf16[512,2048]{1,0:T(8,128)(2,1)}, u32[]{:S(2)}) copy-start(bf16[512,2048]{1,0:T(8,128)(2,1)} %all-gather.2.cloned.1.call-done) | copy-start | bytes 6291460
  61.0 15.8 %copy-start.9 = (bf16[2048,512]{1,0:T(8,128)(2,1)S(1)}, bf16[2048,512]{1,0:T(8,128)(2,1)}, u32[]{:S(2)}) copy-start(bf16[2048,512]{1,0:T(8,128)(2,1)} %param.11) | copy-start | bytes 6291460
  61.0 83.8 %collective-permute-start.2 = (bf16[512,512]{1,0:T(8,128)(2,1)S(1)}, bf16[512,512]{1,0:T(8,128)(2,1)}, u32[]{:S(2)}, u32[]{:S(2)}) collective-permute-start(bf16[512,512]{1,0:T(8,128)(2,1)S(1)} %convolution_convert_fusion.1), channel_id=1, source_target_pairs={{0,8},{4,12},{8,16},{12,20},{16,24},{20,28},{1,9},{5,13},{9,17},{1... | collective-permute-start | bytes 1572872 | tf_op jit(solution)/shard_map/ppermute | solution.py:10
  65.3 79.5 %collective-permute-start.3 = (bf16[512,512]{1,0:T(8,128)(2,1)S(1)}, bf16[512,512]{1,0:T(8,128)(2,1)}, u32[]{:S(2)}, u32[]{:S(2)}) collective-permute-start(bf16[512,512]{1,0:T(8,128)(2,1)S(1)} %convolution_convert_fusion.1), channel_id=1, source_target_pairs={{0,4},{4,8},{8,12},{12,16},{16,20},{20,24},{24,28},{1,5},{5,9},{9,... | collective-permute-start | bytes 1572872 | tf_op jit(solution)/shard_map/ppermute | solution.py:10
  69.4 11.7 %copy-start.3 = (f32[4,128]{1,0:T(4,128)S(1)}, f32[4,128]{1,0:T(4,128)}, u32[]{:S(2)}) copy-start(f32[4,128]{1,0:T(4,128)} %param.17) | copy-start | bytes 6148
  69.4 97.3 %collective-permute-start = (bf16[512,512]{1,0:T(8,128)(2,1)}, bf16[512,512]{1,0:T(8,128)(2,1)}, u32[]{:S(2)}, u32[]{:S(2)}) collective-permute-start(bf16[512,512]{1,0:T(8,128)(2,1)} %convolution_convert_fusion.3), channel_id=1, source_target_pairs={{0,8},{4,12},{8,16},{12,20},{16,24},{20,28},{1,9},{5,13},{9,17},{1... | collective-permute-start | bytes 1572872 | tf_op jit(solution)/shard_map/ppermute | solution.py:10
  72.8 94.0 %collective-permute-start.1 = (bf16[512,512]{1,0:T(8,128)(2,1)}, bf16[512,512]{1,0:T(8,128)(2,1)}, u32[]{:S(2)}, u32[]{:S(2)}) collective-permute-start(bf16[512,512]{1,0:T(8,128)(2,1)} %convolution_convert_fusion.3), channel_id=1, source_target_pairs={{0,4},{4,8},{8,12},{12,16},{16,20},{20,24},{24,28},{1,5},{5,9},{9,... | collective-permute-start | bytes 1572872 | tf_op jit(solution)/shard_map/ppermute | solution.py:10
  135.1 9.7 %copy-start.1 = (f32[512,4,128]{2,0,1:T(8,128)S(1)}, f32[512,4,128]{2,0,1:T(8,128)}, u32[]{:S(2)}) copy-start(f32[512,4,128]{2,0,1:T(8,128)} %copy.16) | copy-start | bytes 3145732
  135.1 9.7 %copy-start.4 = (f32[4,128]{1,0:T(4,128)S(1)}, f32[4,128]{1,0:T(4,128)}, u32[]{:S(2)}) copy-start(f32[4,128]{1,0:T(4,128)} %param.16) | copy-start | bytes 6148
  182.9 43.4 %copy-start.2 = (bf16[512,512]{1,0:T(8,128)(2,1)S(1)}, bf16[512,512]{1,0:T(8,128)(2,1)}, u32[]{:S(2)}) copy-start(bf16[512,512]{1,0:T(8,128)(2,1)} %param.10) | copy-start | bytes 1572868
  185.6 62.1 %copy-start.5 = (f32[512]{0:T(512)S(1)}, f32[512]{0:T(512)}, u32[]{:S(2)}) copy-start(f32[512]{0:T(512)} %param.19) | copy-start | bytes 6148
  185.6 62.1 %copy-start.6 = (f32[512]{0:T(512)S(1)}, f32[512]{0:T(512)}, u32[]{:S(2)}) copy-start(f32[512]{0:T(512)} %param.18) | copy-start | bytes 6148
Sparse Core Ops, SparseCore 0:
  8.9 48.3 all-gather.1
  185.7 40.5 reduce-scatter.1
where the time goes:
time: 257 us
  waiting for transfers between devices  62.8 us (24%)
  local copies, waits for them, and re-layouts  60.4 us (24%)
  matrix products  45.7 us (18%)
  other arithmetic  41.6 us (16%)
  blocking collectives  18.7 us (7%)
  starting transfers between devices  13.8 us (5%)
  between operations  13.6 us (5%)
    reduce_scatter x1, waiting for transfers between devices, shards(): lax.psum_scatter(partial_out.astype(jnp.bfloat16), 'tp', scatter_dimensio...  40.8 us
    another operation x1, other arithmetic  23.2 us
    all_gather x1, waiting for transfers between devices, shards(): own = lax.all_gather(hidden_in, 'tp', axis=1, tiled=True)  21.3 us
    unnamed x23, local copies, waits for them, and re-layouts  20.3 us
    reshape x1, local copies, waits for them, and re-layouts, shift_rows(): flat = padded.reshape(heads, seg * (span + 1))  15 us
    ppermute x4, starting transfers between devices, shifted(): return lax.ppermute(block, axis, route)  13.8 us
    dot_general x1, matrix products, shards(): jnp.einsum('ihd,jhd->hij', content_q, keys, preferred_element_type=jnp.fl...  11.5 us
    dot_general x1, matrix products, shards(): jnp.einsum('hij,jhd->ihd', probs, values, preferred_element_type=jnp.floa...  10.9 us
  transfers between devices with their start and end apart: 6, of which 2 were waited for; matrix products, arithmetic and copies ran while one was open for 47% of the time, Pallas kernels for 0%

commit v1 on v0

--- a/solution.py
+++ b/solution.py
@@ -36,7 +36,14 @@
     span = 3 * seg
     memory = 2 * seg
     place = lax.axis_index("seq")
-    own = lax.all_gather(hidden_in, "tp", axis=1, tiled=True)
+    count = lax.axis_size("tp")
+    right = [(i_2, (i_2 + 1) % count) for i_2 in range(count)]
+    parts = [hidden_in]
+    for far in range(1, count):
+        parts = [lax.ppermute(parts[0], "tp", right), *parts]
+    whole = jnp.concatenate(parts, axis=1)
+    places = (lax.axis_index("tp") + 1) * parts[-1].shape[1]
+    own = jnp.roll(whole, places, axis=1)
     query = jnp.dot(own, w_query, preferred_element_type=jnp.float32).astype(jnp.bfloat16)
     own_keys = jnp.dot(own, w_key, preferred_element_type=jnp.float32).astype(jnp.bfloat16)
     own_values = jnp.dot(own, w_value, preferred_element_type=jnp.float32).astype(jnp.bfloat16)

time: 257 us -> 274 us (1.066)
  local copies, waits for them, and re-layouts: 60.4 us -> 69.8 us
  starting transfers between devices: 13.8 us -> 17.7 us
  matrix products: 45.7 us -> 48.8 us
    ppermute x0 -> x3, waiting for transfers between devices: none -> 22.8 us  [shards(): parts = [lax.ppermute(parts[0], 'tp', right), *parts]]
    all_gather x1 -> x0, waiting for transfers between devices: 21.3 us -> none  [shards(): own = lax.all_gather(hidden_in, 'tp', axis=1, tiled=True)]
    unnamed x23 -> x32, local copies, waits for them, and re-layouts: 20.3 us -> 25.8 us
    ppermute x0 -> x3, starting transfers between devices: none -> 4.68 us  [shards(): parts = [lax.ppermute(parts[0], 'tp', right), *parts]]
    dot_general x1, matrix products: 11.5 us -> 16 us  [shards(): jnp.einsum('ihd,jhd->hij', content_q, keys, preferred_element_type=jnp.fl...]
    slice x1, local copies, waits for them, and re-layouts: 9.66 us -> 13.3 us  [shift_rows(): return flat[:, seg - 1:seg - 1 + seg * span].reshape(heads, seg, span)]
  transfers between devices with their start and end apart: 6 -> 8, of which waited for: 2 -> 3; matrix products, arithmetic and copies ran while one was open for 47% -> 39% of each run, Pallas kernels for 0% -> 0%
where the time goes in v1:
time: 274 us; the launch traced here: 273 us
  local copies, waits for them, and re-layouts  69.8 us (25%)
  waiting for transfers between devices  62.5 us (23%)
  matrix products  48.8 us (18%)
  other arithmetic  41.6 us (15%)
  blocking collectives  18.7 us (7%)
  starting transfers between devices  17.7 us (6%)
  between operations  13.6 us (5%)
    reduce_scatter x1, waiting for transfers between devices, shards(): lax.psum_scatter(partial_out.astype(jnp.bfloat16), 'tp', scatter_dimensio...  39.6 us
    unnamed x32, local copies, waits for them, and re-layouts  25.8 us
    another operation x1, other arithmetic  23.2 us
    ppermute x3, waiting for transfers between devices, shards(): parts = [lax.ppermute(parts[0], 'tp', right), *parts]  22.8 us
    dot_general x1, matrix products, shards(): jnp.einsum('ihd,jhd->hij', content_q, keys, preferred_element_type=jnp.fl...  16 us
    reshape x1, local copies, waits for them, and re-layouts, shift_rows(): flat = padded.reshape(heads, seg * (span + 1))  15 us
    slice x1, local copies, waits for them, and re-layouts, shift_rows(): return flat[:, seg - 1:seg - 1 + seg * span].reshape(heads, seg, span)  13.3 us
    ppermute x4, starting transfers between devices, shifted(): return lax.ppermute(block, axis, route)  13 us
  transfers between devices with their start and end apart: 8, of which 3 were waited for; matrix products, arithmetic and copies ran while one was open for 39% of the time, Pallas kernels for 0%

profile of v1, /device:TPU:0, one launch (start us, length us, event | category | flops | bytes accessed | tf_op | source)
XLA Modules:
  0.0 272.9 jit_solution(7249034505649833546)
XLA Ops:
  6.5 3.1 %collective-permute-start = (bf16[512,512]{1,0:T(8,128)(2,1)}, bf16[512,512]{1,0:T(8,128)(2,1)S(1)}, u32[]{:S(2)}, u32[]{:S(2)}) collective-permute-start(bf16[512,512]{1,0:T(8,128)(2,1)} %param.10), channel_id=1, source_target_pairs={{0,1},{1,2},{2,3},{3,0},{4,5},{5,6},{6,7},{7,4},{8,9},{9,10},{10,1... | collective-permute-start | bytes 1572872 | tf_op jit(solution)/shard_map/ppermute | solution.py:43
  9.6 23.2 %fusion.3 = (bf16[1536,1024]{1,0:T(8,128)(2,1)S(1)}, bf16[1536,1024]{1,0:T(8,128)(2,1)S(1)}) fusion(f32[1024]{0:T(1024)S(1)} %multiply_exponential_fusion, f32[1536]{0:T(1024)S(1)} %subtract_convert_fusion), kind=kLoop, calls=%fused_computation.8 | loop fusion | flops 4718592 | bytes 6301696 | tf_op jit(solution)/shard_map/convert.1
  32.9 1.6 collective-permute-start.1
  34.5 4.9 %fusion.11 = bf16[1536,512]{0,1:T(8,128)(2,1)} fusion(bf16[2048,512]{1,0:T(8,128)(2,1)S(1)} %copy-done.8, bf16[1536,1024]{1,0:T(8,128)(2,1)S(1)} %get-tuple-element.6, bf16[1536,1024]{1,0:T(8,128)(2,1)S(1)} %get-tuple-element.5), kind=kOutput, calls=%fused_computation.17 | convolution fusion | flops 3234594816 | bytes 9961472 | tf_op jit(solution)/shard_map/dot_general | solution.py:58
  39.4 8.8 %collective-permute-done.1 = bf16[512,512]{1,0:T(8,128)(2,1)} collective-permute-done((bf16[512,512]{1,0:T(8,128)(2,1)S(1)}, bf16[512,512]{1,0:T(8,128)(2,1)}, u32[]{:S(2)}, u32[]{:S(2)}) %collective-permute-start.1) | collective-permute-done | bytes 524320 | tf_op jit(solution)/shard_map/ppermute | solution.py:43
  48.9 14.0 %collective-permute-done.2 = bf16[512,512]{1,0:T(8,128)(2,1)} collective-permute-done((bf16[512,512]{1,0:T(8,128)(2,1)}, bf16[512,512]{1,0:T(8,128)(2,1)}, u32[]{:S(2)}, u32[]{:S(2)}) %collective-permute-start.2) | collective-permute-done | bytes 524320 | tf_op jit(solution)/shard_map/ppermute | solution.py:43
  65.1 1.1 constant_dynamic-update-slice_fusion.5
  68.6 2.0 fusion.22
  70.7 2.2 collective-permute-start.4
  72.9 4.1 %collective-permute-start.3 = (bf16[512,512]{1,0:T(8,128)(2,1)}, bf16[512,512]{1,0:T(8,128)(2,1)}, u32[]{:S(2)}, u32[]{:S(2)}) collective-permute-start(bf16[512,512]{1,0:T(8,128)(2,1)} %fusion.22), channel_id=1, source_target_pairs={{0,8},{4,12},{8,16},{12,20},{16,24},{20,28},{1,9},{5,13},{9,17},{1... | collective-permute-start | bytes 1572872 | tf_op jit(solution)/shard_map/ppermute | solution.py:10
  77.0 2.1 fusion.28
  79.0 4.1 %collective-permute-start.6 = (bf16[512,512]{1,0:T(8,128)(2,1)}, bf16[512,512]{1,0:T(8,128)(2,1)}, u32[]{:S(2)}, u32[]{:S(2)}) collective-permute-start(bf16[512,512]{1,0:T(8,128)(2,1)} %fusion.28), channel_id=1, source_target_pairs={{0,4},{4,8},{8,12},{12,16},{16,20},{20,24},{24,28},{1,5},{5,9},{9,... | collective-permute-start | bytes 1572872 | tf_op jit(solution)/shard_map/ppermute | solution.py:10
  83.2 2.6 collective-permute-start.5
  85.8 2.1 fusion.25
  87.9 2.2 copy.16
  90.1 8.1 %fusion.34 = f32[4,512,1536]{2,1,0:T(8,128)} fusion(bf16[1536,4,128]{0,2,1:T(8,128)(2,1)} %bitcast.32, f32[512,4,128]{2,0,1:T(8,128)} %copy.16, f32[4,128]{1,0:T(4,128)S(1)} %copy-done.4), kind=kOutput, calls=%fused_computation.40 | convolution fusion | flops 805830656 | bytes 15206400 | tf_op jit(solution)/shard_map/ihd,ehd->hie/dot_general | solution.py:68
  98.2 10.8 %pad.4 = f32[4,512,1537]{2,1,0:T(8,128)} pad(f32[4,512,1536]{2,1,0:T(8,128)} %fusion.34, f32[]{:T(128)} %constant.59.clone.1), padding=0_0x0_0x0_1 | pad | bytes 25174020 | tf_op jit(solution)/shard_map/jit(_pad)/pad | solution.py:23
  109.0 20.2 %reshape.101 = f32[3147776]{0:T(1024)} reshape(f32[4,512,1537]{2,1,0:T(8,128)} %pad.4) | data formatting | bytes 25182208
  129.1 15.0 %reshape.96 = f32[4,786944]{1,0:T(4,128)} reshape(f32[3147776]{0:T(1024)} %reshape.101) | data formatting | bytes 25182208 | tf_op jit(solution)/shard_map/reshape | solution.py:24
  144.2 13.3 %slice.4 = f32[4,786432]{1,0:T(4,128)} slice(f32[4,786944]{1,0:T(4,128)} %reshape.96), slice={[0:4], [511:786943]} | slice | bytes 25165824 | tf_op jit(solution)/shard_map/slice | solution.py:25
  157.5 2.6 pad_maximum_fusion
  160.1 2.6 copy.22
  162.8 16.0 %fusion.2 = f32[4,512,1536]{2,1,0:T(8,128)} fusion(f32[1,4,512,1536]{3,1,2,0:T(4,128)} %bitcast.31, pred[512,1536]{1,0:T(8,128)(4,1)S(1)} %fusion.10, f32[512,4,128]{2,0,1:T(8,128)} %copy.16, f32[4,128]{1,0:T(4,128)S(1)} %copy-done.5, bf16[512,512]{1,0:T(8,128)(2,1)} %fusion.28, bf16[512,512]{1,0:T(8,128)(2,1)} %collective-permute-done.6, ...), kind=kOutput, calls=%fused_computation.3 | convolution fusion | flops 819986432 | bytes 28575744 | tf_op jit(solution)/shard_map/ihd,jhd->hij/dot_general | solution.py:67
  178.8 10.5 %fusion.42 = f32[4,512]{1,0:T(4,128)S(1)} fusion(f32[4,512,1536]{2,1,0:T(8,128)} %fusion.2), kind=kOutput, calls=%fused_computation.62 | output fusion | flops 6292991 | bytes 12591104 | tf_op jit(solution)/shard_map/sub | solution.py:75
  189.2 11.0 %fusion.31 = bf16[4,128,512]{2,1,0:T(8,128)(2,1)S(1)} fusion(bf16[1536,4,128]{0,2,1:T(8,128)(2,1)} %bitcast.33, f32[4,512]{1,0:T(4,128)S(1)} %fusion.42, f32[4,512,1536]{2,1,0:T(8,128)} %fusion.2), kind=kOutput, calls=%fused_computation.32 | convolution fusion | flops 815009280 | bytes 14688256 | tf_op jit(solution)/shard_map/hij,jhd->ihd/dot_general | solution.py:76
  200.3 2.6 convolution_convert_fusion
  203.0 39.6 %reduce-scatter.2.cloned.1.call-done = bf16[512,512]{1,0:T(8,128)(2,1)} async-done(((bf16[512,2048]{1,0:T(8,128)(2,1)}), bf16[512,512]{1,0:T(8,128)(2,1)}) %reduce-scatter.2.cloned.1.call-update) | async-done | bytes 524304 | tf_op jit(solution)/shard_map/reduce_scatter | solution.py:79
  242.6 1.2 fusion.33
  243.9 10.2 %psum.14 = f32[512]{0:T(512)S(1)} all-reduce(f32[512]{0:T(512)S(1)} %fusion.33), channel_id=1, replica_groups=mesh['seq'=8,'tp'=4] {'tp'}, use_global_device_ids=true, to_apply=%region_4.5 | all-reduce | flops 512 | bytes 4096 | tf_op jit(solution)/shard_map/psum | solution.py:83
  254.0 1.3 multiply_reduce_fusion
  255.4 8.6 %psum.15 = f32[512]{0:T(512)S(1)} all-reduce(f32[512]{0:T(512)S(1)} %multiply_reduce_fusion), channel_id=1, replica_groups=mesh['seq'=8,'tp'=4] {'tp'}, use_global_device_ids=true, to_apply=%region_6.7 | all-reduce | flops 512 | bytes 4096 | tf_op jit(solution)/shard_map/psum | solution.py:86
  264.0 2.1 add_convert_fusion
  (46 shorter events, 5.3 us)
Async XLA Ops:
  6.5 193.7 %copy-start = (bf16[512,2048]{1,0:T(8,128)(2,1)S(1)}, bf16[512,2048]{1,0:T(8,128)(2,1)}, u32[]{:S(2)}) copy-start(bf16[512,2048]{1,0:T(8,128)(2,1)} %param.15) | copy-start | bytes 6291460
  6.5 236.1 %reduce-scatter.2.cloned.1.call-start = ((), (), s32[]{:S(2)}) async-start(), calls=%async_computation.1 | async-start | bytes 2621440 | tf_op jit(solution)/shard_map/reduce_scatter | solution.py:79
  6.5 26.3 %collective-permute-start = (bf16[512,512]{1,0:T(8,128)(2,1)}, bf16[512,512]{1,0:T(8,128)(2,1)S(1)}, u32[]{:S(2)}, u32[]{:S(2)}) collective-permute-start(bf16[512,512]{1,0:T(8,128)(2,1)} %param.10), channel_id=1, source_target_pairs={{0,1},{1,2},{2,3},{3,0},{4,5},{5,6},{6,7},{7,4},{8,9},{9,10},{10,1... | collective-permute-start | bytes 1572872 | tf_op jit(solution)/shard_map/ppermute | solution.py:43
  9.6 24.9 %copy-start.8 = (bf16[2048,512]{1,0:T(8,128)(2,1)S(1)}, bf16[2048,512]{1,0:T(8,128)(2,1)}, u32[]{:S(2)}) copy-start(bf16[2048,512]{1,0:T(8,128)(2,1)} %param.14) | copy-start | bytes 6291460
  32.9 6.5 %copy-start.2 = (bf16[512,512]{1,0:T(8,128)(2,1)}, bf16[512,512]{1,0:T(8,128)(2,1)S(1)}, u32[]{:S(2)}) copy-start(bf16[512,512]{1,0:T(8,128)(2,1)S(1)} %collective-permute-done) | copy-start | bytes 1572868
  32.9 15.3 %collective-permute-start.1 = (bf16[512,512]{1,0:T(8,128)(2,1)S(1)}, bf16[512,512]{1,0:T(8,128)(2,1)}, u32[]{:S(2)}, u32[]{:S(2)}) collective-permute-start(bf16[512,512]{1,0:T(8,128)(2,1)S(1)} %collective-permute-done), channel_id=1, source_target_pairs={{0,1},{1,2},{2,3},{3,0},{4,5},{5,6},{6,7},{7,4},{8,9},{9,10},{10,1... | collective-permute-start | bytes 1572872 | tf_op jit(solution)/shard_map/ppermute | solution.py:43
  39.4 26.8 %copy-start.1 = (bf16[512,512]{1,0:T(8,128)(2,1)S(1)}, bf16[512,512]{1,0:T(8,128)(2,1)}, u32[]{:S(2)}) copy-start(bf16[512,512]{1,0:T(8,128)(2,1)} %param.10) | copy-start | bytes 1572868
  48.2 14.6 %collective-permute-start.2 = (bf16[512,512]{1,0:T(8,128)(2,1)}, bf16[512,512]{1,0:T(8,128)(2,1)}, u32[]{:S(2)}, u32[]{:S(2)}) collective-permute-start(bf16[512,512]{1,0:T(8,128)(2,1)} %collective-permute-done.1), channel_id=1, source_target_pairs={{0,1},{1,2},{2,3},{3,0},{4,5},{5,6},{6,7},{7,4},{8,9},{9,10},{10,1... | collective-permute-start | bytes 1572872 | tf_op jit(solution)/shard_map/ppermute | solution.py:43
  48.3 20.2 %copy-start.3 = (bf16[512,512]{1,0:T(8,128)(2,1)S(1)}, bf16[512,512]{1,0:T(8,128)(2,1)}, u32[]{:S(2)}) copy-start(bf16[512,512]{1,0:T(8,128)(2,1)} %copy-done.2) | copy-start | bytes 1572868
  48.8 19.8 %copy-start.9 = (bf16[2048,512]{1,0:T(8,128)(2,1)S(1)}, bf16[2048,512]{1,0:T(8,128)(2,1)}, u32[]{:S(2)}) copy-start(bf16[2048,512]{1,0:T(8,128)(2,1)} %param.13) | copy-start | bytes 6291460
  68.5 8.4 %copy-start.10 = (bf16[2048,512]{1,0:T(8,128)(2,1)S(1)}, bf16[2048,512]{1,0:T(8,128)(2,1)}, u32[]{:S(2)}) copy-start(bf16[2048,512]{1,0:T(8,128)(2,1)} %param.12) | copy-start | bytes 6291460
  70.7 15.1 %copy-start.11 = (bf16[2048,512]{1,0:T(8,128)(2,1)S(1)}, bf16[2048,512]{1,0:T(8,128)(2,1)}, u32[]{:S(2)}) copy-start(bf16[2048,512]{1,0:T(8,128)(2,1)} %param.11) | copy-start | bytes 6291460
  70.7 86.8 %collective-permute-start.4 = (bf16[512,512]{1,0:T(8,128)(2,1)}, bf16[512,512]{1,0:T(8,128)(2,1)}, u32[]{:S(2)}, u32[]{:S(2)}) collective-permute-start(bf16[512,512]{1,0:T(8,128)(2,1)} %fusion.22), channel_id=1, source_target_pairs={{0,4},{4,8},{8,12},{12,16},{16,20},{20,24},{24,28},{1,5},{5,9},{9,... | collective-permute-start | bytes 1572872 | tf_op jit(solution)/shard_map/ppermute | solution.py:10
  72.9 84.6 %collective-permute-start.3 = (bf16[512,512]{1,0:T(8,128)(2,1)}, bf16[512,512]{1,0:T(8,128)(2,1)}, u32[]{:S(2)}, u32[]{:S(2)}) collective-permute-start(bf16[512,512]{1,0:T(8,128)(2,1)} %fusion.22), channel_id=1, source_target_pairs={{0,8},{4,12},{8,16},{12,20},{16,24},{20,28},{1,9},{5,13},{9,17},{1... | collective-permute-start | bytes 1572872 | tf_op jit(solution)/shard_map/ppermute | solution.py:10
  79.0 11.1 %copy-start.4 = (f32[4,128]{1,0:T(4,128)S(1)}, f32[4,128]{1,0:T(4,128)}, u32[]{:S(2)}) copy-start(f32[4,128]{1,0:T(4,128)} %param.17) | copy-start | bytes 6148
  79.0 83.7 %collective-permute-start.6 = (bf16[512,512]{1,0:T(8,128)(2,1)}, bf16[512,512]{1,0:T(8,128)(2,1)}, u32[]{:S(2)}, u32[]{:S(2)}) collective-permute-start(bf16[512,512]{1,0:T(8,128)(2,1)} %fusion.28), channel_id=1, source_target_pairs={{0,4},{4,8},{8,12},{12,16},{16,20},{20,24},{24,28},{1,5},{5,9},{9,... | collective-permute-start | bytes 1572872 | tf_op jit(solution)/shard_map/ppermute | solution.py:10
  83.2 79.6 %collective-permute-start.5 = (bf16[512,512]{1,0:T(8,128)(2,1)}, bf16[512,512]{1,0:T(8,128)(2,1)}, u32[]{:S(2)}, u32[]{:S(2)}) collective-permute-start(bf16[512,512]{1,0:T(8,128)(2,1)} %fusion.28), channel_id=1, source_target_pairs={{0,8},{4,12},{8,16},{12,20},{16,24},{20,28},{1,9},{5,13},{9,17},{1... | collective-permute-start | bytes 1572872 | tf_op jit(solution)/shard_map/ppermute | solution.py:10
  157.5 5.3 %copy-start.5 = (f32[4,128]{1,0:T(4,128)S(1)}, f32[4,128]{1,0:T(4,128)}, u32[]{:S(2)}) copy-start(f32[4,128]{1,0:T(4,128)} %param.16) | copy-start | bytes 6148
  200.3 63.7 %copy-start.6 = (f32[512]{0:T(512)S(1)}, f32[512]{0:T(512)}, u32[]{:S(2)}) copy-start(f32[512]{0:T(512)} %param.19) | copy-start | bytes 6148
  200.3 63.7 %copy-start.7 = (f32[512]{0:T(512)S(1)}, f32[512]{0:T(512)}, u32[]{:S(2)}) copy-start(f32[512]{0:T(512)} %param.18) | copy-start | bytes 6148
Sparse Core Ops, SparseCore 0:
  203.1 39.4 reduce-scatter.1
